TPU v7x, 1024 devices: a whole 4x8x16 slice. The times are simulated.
1024 devices in a mesh: group: 16 (over y, core), member: 64 (over z, x).
Axes of the slice: x: 4, y: 8, z: 16, core: 2. Of those that a mesh axis runs over, the one named last changes fastest.
Arguments:
- off_tiles: bfloat16 [2048, 8, 128, 128], P(('group', 'member')), may hold values from -0.1875 to 0.1875
- off_cols: int32 [2048, 8], P(('group', 'member')), may hold values from 0 to 73
- member_send: int32 [1024, 64, 1], P(('group', 'member')), may hold values from 0 to 1
- group_send: int32 [1024, 4], P(('group', 'member')), may hold values from 0 to 1
- diag_tiles: bfloat16 [2048, 128, 128], P(('group', 'member')), may hold values from -1 to 9
- smoother: bfloat16 [2048, 128, 128], P(('group', 'member')), may hold values from -1 to 1
- agg_map: int32 [2048], P(('group', 'member')), may hold values from 0 to 1
- prolong: bfloat16 [2048, 128, 128], P(('group', 'member')), may hold values from -0.5 to 0.5
- coarse_inv: bfloat16 [4096, 4096], P(None, 'group'), may hold values from -0.005859375 to 0.005859375
- krylov_basis: bfloat16 [2048, 32, 128], P(('group', 'member')), may hold values from -24 to 24, as said below
Outputs:
- preconditioned: bfloat16 [2048, 8, 128], P(('group', 'member'))
- coefficients: float32 [32, 8], replicated
- gram_matrix: float32 [8, 8], replicated
- new_block: float32 [2048, 8, 128], P(('group', 'member'))
Inputs may be any that keep to these rules, and one draw needn't show every extreme that they name: `off_cols`: entries below 2 name the device's own row tiles; entry 2 + p + s names slot s of what member p of the same group sends; the last 8 entries name what the groups below and above send. `member_send`: entry [d, p, s] is the local row tile that device d sends to member p of its group in slot s. `group_send`: entry [d, s] is the local row tile that device d sends, in slot s, to the same member of the groups below and above. `krylov_basis`: the 32 basis vectors are orthonormal, up to bfloat16 rounding, under the inner product (1 / 262144) times the sum over all rows.
All inputs are finite; a program needn't handle non-finite values.
Results may differ from a plain program's by a relative error of at most 0.02.
Values may be sent and summed in bfloat16 or wider, within the bound.
A program may use at most 32 MiB of HBM per device.

v0:
```python
import jax
import jax.numpy as jnp
from jax import lax
from jax.sharding import Mesh
from jax.sharding import PartitionSpec as P

TILE = 128
NVEC = 8
GH = 1
CTG = 2
MEMBER = ("member_0", "member_1")
GROUP = ("group_0", "group_1")
GROUP_MEMBER = ("group_0", "group_1", "member_0", "member_1")


def extended_2(cells, sides, width):
    for axis, dim in sides:
        count = lax.axis_size(axis)
        ends = count - 1
        head = lax.slice_in_dim(cells, 0, width, axis=dim)
        tail = lax.slice_in_dim(cells, cells.shape[dim] - width, cells.shape[dim], axis=dim)
        cells = jnp.concatenate(
            [
                lax.ppermute(tail, axis, [(i, (i + 1) % count) for i in range(ends)]),
                cells,
                lax.ppermute(head, axis, [((i + 1) % count, i) for i in range(ends)]),
            ],
            axis=dim,
        )
    return cells


def over_axes(shard, axes):
    for axis in axes:
        shard = lax.psum(shard, axis)
    return shard


def in_order(pieces, dim):
    shape = list(pieces.shape[1:])
    shape[dim] *= pieces.shape[0]
    return jnp.moveaxis(pieces, 0, dim).reshape(shape)


def from_everyone(shard, axis):
    copies = jnp.broadcast_to(shard, (lax.axis_size(axis), *shard.shape))
    return lax.all_to_all(copies, axis, split_axis=0, concat_axis=0, tiled=True)


def gathered_copies(shard, axis, dim):
    return in_order(from_everyone(shard, axis), dim)


def extend_tiles(values, member_send, group_send, members):
    outgoing = values[member_send[0].reshape(-1)].reshape(members, GH, NVEC, TILE)
    arrived = lax.all_to_all(outgoing, MEMBER, split_axis=0, concat_axis=0, tiled=True).reshape(
        members * GH, NVEC, TILE
    )
    rim_tiles = values[group_send[0]][None]
    beside = extended_2(rim_tiles, ((GROUP, 0),), 1)
    return jnp.concatenate([values, arrived, beside[0], beside[2]], axis=0)


def operate(values, off_tiles, off_cols, diag_tiles, member_send, group_send, members):
    extended = extend_tiles(values, member_send, group_send, members)
    picked = extended[off_cols]
    far_part = jnp.einsum("tkcj,tkji->tci", picked, off_tiles, preferred_element_type=jnp.float32)
    near_part = jnp.einsum("tcj,tji->tci", values, diag_tiles, preferred_element_type=jnp.float32)
    return near_part + far_part


def tilewise(left_side, tiles):
    return jnp.einsum("tcj,tji->tci", left_side, tiles, preferred_element_type=jnp.float32)


def exact_product(form, first_operand, second_operand):
    return jnp.einsum(form, first_operand, second_operand)


def local(
    off_tiles,
    off_cols,
    member_send,
    group_send,
    diag_tiles,
    smoother,
    agg_map,
    prolong,
    coarse_inv,
    krylov_basis,
):
    members = lax.axis_size(MEMBER)
    groups = lax.axis_size(GROUP)
    tiles_dev = diag_tiles.shape[0]
    rows_all = tiles_dev * TILE * members * groups
    scale_rows = 1.0 / rows_all

    def apply_operator(values):
        return operate(values, off_tiles, off_cols, diag_tiles, member_send, group_send, members)

    last_block = krylov_basis[:, krylov_basis.shape[1] - NVEC :, :]
    block_wide = last_block.astype(jnp.float32)
    first = tilewise(last_block, smoother).astype(jnp.bfloat16)
    residual_one = (block_wide - apply_operator(first)).astype(jnp.bfloat16)
    pieces = jnp.einsum("tci,tji->tcj", residual_one, prolong, preferred_element_type=jnp.float32)
    selector = (agg_map[:, None] == jnp.arange(CTG, dtype=jnp.int32)[None, :]).astype(jnp.float32)
    coarse_part = exact_product("ta,tcj->acj", selector, pieces)
    group_sum = over_axes(coarse_part, MEMBER)
    coarse_all = gathered_copies(group_sum, GROUP, 0)
    coarse_round = coarse_all.astype(jnp.bfloat16)
    columns = coarse_inv.reshape(groups * CTG, TILE, CTG * TILE)
    correction = jnp.einsum(
        "acj,ajo->co", coarse_round, columns, preferred_element_type=jnp.float32
    )
    correction = correction.astype(jnp.bfloat16).reshape(NVEC, CTG, TILE)
    chosen = jnp.einsum(
        "ta,cak->tck", selector.astype(jnp.bfloat16), correction, preferred_element_type=jnp.float32
    )
    second = (first.astype(jnp.float32) + tilewise(chosen.astype(jnp.bfloat16), prolong)).astype(
        jnp.bfloat16
    )
    residual_two = (block_wide - apply_operator(second)).astype(jnp.bfloat16)
    preconditioned = (second.astype(jnp.float32) + tilewise(residual_two, smoother)).astype(
        jnp.bfloat16
    )
    applied = apply_operator(preconditioned).astype(jnp.bfloat16)
    coeff_part = (
        jnp.einsum("tpi,tci->pc", krylov_basis, applied, preferred_element_type=jnp.float32)
        * scale_rows
    )
    basis_wide = krylov_basis.astype(jnp.float32)
    self_part = (
        jnp.einsum("tci,tdi->cd", applied, applied, preferred_element_type=jnp.float32) * scale_rows
    )
    basis_part = (
        jnp.einsum("tpi,tqi->pq", krylov_basis, krylov_basis, preferred_element_type=jnp.float32)
        * scale_rows
    )
    coefficients, self_total, basis_total = (
        over_axes(coeff_part, GROUP_MEMBER),
        over_axes(self_part, GROUP_MEMBER),
        over_axes(basis_part, GROUP_MEMBER),
    )
    remainder = applied.astype(jnp.float32) - exact_product("pc,tpi->tci", coefficients, basis_wide)
    cross = exact_product("pc,pd->cd", coefficients, coefficients)
    weighted = exact_product("pq,qd->pd", basis_total, coefficients)
    gram_matrix = self_total - 2.0 * cross + exact_product("pc,pd->cd", coefficients, weighted)
    factor = jnp.linalg.cholesky(gram_matrix)
    inverse = lax.linalg.triangular_solve(
        factor, jnp.eye(NVEC, dtype=jnp.float32), left_side=True, lower=True
    )
    new_block = exact_product("cd,tdi->tci", inverse, remainder)
    return (preconditioned, coefficients, gram_matrix, new_block)


def solution(mesh):
    torus = Mesh(mesh.devices.reshape(8, 2, 16, 4), ("group_0", "group_1", "member_0", "member_1"))
    in_specs = (
        P(GROUP_MEMBER, None, None, None),
        P(GROUP_MEMBER, None),
        P(GROUP_MEMBER, None, None),
        P(GROUP_MEMBER, None),
        P(GROUP_MEMBER, None, None),
        P(GROUP_MEMBER, None, None),
        P(GROUP_MEMBER),
        P(GROUP_MEMBER, None, None),
        P(None, GROUP),
        P(GROUP_MEMBER, None, None),
    )
    out_specs = (P(GROUP_MEMBER, None, None), P(), P(), P(GROUP_MEMBER, None, None))
    return jax.shard_map(local, mesh=torus, in_specs=in_specs, out_specs=out_specs, check_vma=False)
```

profile of v0, /device:TPU:8, one launch (start us, length us, event | category | flops | bytes accessed | tf_op | source)
XLA Modules:
  0.0 254.6 jit_solution(14537969134938007828)
XLA Ops:
  0.6 0.0 copy-start
  0.6 0.0 copy-start.5
  0.7 0.0 copy-start.9
  0.7 0.8 fusion.40
  1.5 1.0 convolution_convert_fusion
  2.5 1.3 gather_fusion
  3.7 22.2 %all-to-all-start = ((bf16[64,1,8,128]{3,2,1,0:T(8,128)(2,1)}), bf16[64,1,8,128]{3,2,1,0:T(8,128)(2,1)S(1)}, u32[]{:S(2)}, u32[]{:S(2)}) async-start(bf16[64,1,8,128]{3,2,1,0:T(8,128)(2,1)} %bitcast.5), calls=%async_computation | async-start | bytes 262144 | tf_op jit(solution)/shard_map/all_to_all | solution.py:56
  26.0 0.7 fusion.41
  26.7 0.6 gather_fusion.1
  27.2 1.9 collective-permute-start
  29.1 3.6 %collective-permute-start.1 = (bf16[1,4,8,128]{3,2,1,0:T(8,128)(2,1)S(1)}, bf16[1,4,8,128]{3,2,1,0:T(8,128)(2,1)S(1)}, u32[]{:S(2)}, u32[]{:S(2)}) collective-permute-start(bf16[1,4,8,128]{3,2,1,0:T(8,128)(2,1)S(1)} %bitcast.143), channel_id=1, source_target_pairs={{64,0},{128,64},{192,128},{256,192},{320,256},{384,320},{448,384},... | collective-permute-start | bytes 24584 | tf_op jit(solution)/shard_map/ppermute | solution.py:26
  32.8 0.7 compare_select_fusion
  33.5 0.1 reshape.126
  33.6 0.0 collective-permute-done
  33.6 0.6 collective-permute-done.1
  34.1 9.5 %all-to-all-done = bf16[64,1,8,128]{3,2,1,0:T(8,128)(2,1)S(1)} async-done(((bf16[64,1,8,128]{3,2,1,0:T(8,128)(2,1)}), bf16[64,1,8,128]{3,2,1,0:T(8,128)(2,1)S(1)}, u32[]{:S(2)}, u32[]{:S(2)}) %all-to-all-start) | async-done | bytes 131104 | tf_op jit(solution)/shard_map/all_to_all | solution.py:56
  43.7 0.6 gather_fusion.2
  44.3 1.3 convolution_bitcast_fusion.6
  45.6 0.0 copy-start.6
  45.6 1.1 fusion.14
  46.7 0.8 fusion.25
  47.5 28.1 %psum.98 = f32[2,8,128]{2,0,1:T(2,128)S(1)} all-reduce(f32[2,8,128]{2,0,1:T(2,128)S(1)} %fusion.25), channel_id=1, replica_groups=mesh['group_0'=8,'group_1'=2,'member_0'=16,'member_1'=4] {'member_0'}, use_global_device_ids=true, to_apply=%region_0.0 | all-reduce | flops 2048 | bytes 16384 | tf_op jit(solution)/shard_map/psum | solution.py:35
  75.7 9.1 %psum.99 = bf16[2,8,128]{2,0,1:T(2,128)(2,1)S(1)} all-reduce(f32[2,8,128]{2,0,1:T(2,128)S(1)} %psum.98), channel_id=1, replica_groups=mesh['group_0'=8,'group_1'=2,'member_0'=16,'member_1'=4] {'member_1'}, use_global_device_ids=true, to_apply=%region_1.0 | all-reduce | flops 2048 | bytes 12288 | tf_op jit(solution)/shard_map/psum | solution.py:35
  84.8 13.9 %all_to_all.20 = bf16[16,2,8,128]{3,2,1,0:T(8,128)(2,1)S(1)} all-to-all(bf16[16,2,8,128]{3,2,1,0:T(8,128)(2,1)S(1)} %broadcast_in_dim.13), channel_id=1, replica_groups=mesh['group_0'=8,'group_1'=2,'member_0'=16,'member_1'=4] {'group_0','gro..., dimensions={0} | all-to-all | bytes 131072 | tf_op jit(solution)/shard_map/all_to_all | solution.py:47
  98.6 0.4 fusion.13
  99.0 0.2 fusion.32
  99.2 0.1 fusion.9
  99.3 1.3 gather_fusion.3
  100.6 6.1 %all-to-all-start.2 = ((bf16[64,1,8,128]{3,2,1,0:T(8,128)(2,1)}), bf16[64,1,8,128]{3,2,1,0:T(8,128)(2,1)S(1)}, u32[]{:S(2)}, u32[]{:S(2)}) async-start(bf16[64,1,8,128]{3,2,1,0:T(8,128)(2,1)} %bitcast.20), calls=%async_computation.2 | async-start | bytes 262144 | tf_op jit(solution)/shard_map/all_to_all | solution.py:56
  106.7 0.6 gather_fusion.4
  107.3 1.9 collective-permute-start.2
  109.2 3.6 %collective-permute-start.3 = (bf16[1,4,8,128]{3,2,1,0:T(8,128)(2,1)S(1)}, bf16[1,4,8,128]{3,2,1,0:T(8,128)(2,1)S(1)}, u32[]{:S(2)}, u32[]{:S(2)}) collective-permute-start(bf16[1,4,8,128]{3,2,1,0:T(8,128)(2,1)S(1)} %bitcast.147), channel_id=1, source_target_pairs={{64,0},{128,64},{192,128},{256,192},{320,256},{384,320},{448,384},... | collective-permute-start | bytes 24584 | tf_op jit(solution)/shard_map/ppermute | solution.py:26
  112.9 1.3 collective-permute-done.3
  114.2 10.6 %all-to-all-done.2 = bf16[64,1,8,128]{3,2,1,0:T(8,128)(2,1)S(1)} async-done(((bf16[64,1,8,128]{3,2,1,0:T(8,128)(2,1)}), bf16[64,1,8,128]{3,2,1,0:T(8,128)(2,1)S(1)}, u32[]{:S(2)}, u32[]{:S(2)}) %all-to-all-start.2) | async-done | bytes 131104 | tf_op jit(solution)/shard_map/all_to_all | solution.py:56
  124.8 0.6 gather_fusion.5
  125.4 0.2 convolution_bitcast_fusion.5
  125.6 0.2 fusion.11
  125.8 1.3 gather_fusion.6
  127.1 4.6 %all-to-all-start.3 = ((bf16[64,1,8,128]{3,2,1,0:T(8,128)(2,1)}), bf16[64,1,8,128]{3,2,1,0:T(8,128)(2,1)S(1)}, u32[]{:S(2)}, u32[]{:S(2)}) async-start(bf16[64,1,8,128]{3,2,1,0:T(8,128)(2,1)} %bitcast.29), calls=%async_computation.3 | async-start | bytes 262144 | tf_op jit(solution)/shard_map/all_to_all | solution.py:56
  131.7 0.6 gather_fusion.7
  132.3 2.3 collective-permute-start.4
  134.6 3.2 %collective-permute-start.5 = (bf16[1,4,8,128]{3,2,1,0:T(8,128)(2,1)S(1)}, bf16[1,4,8,128]{3,2,1,0:T(8,128)(2,1)S(1)}, u32[]{:S(2)}, u32[]{:S(2)}) collective-permute-start(bf16[1,4,8,128]{3,2,1,0:T(8,128)(2,1)S(1)} %bitcast.145), channel_id=1, source_target_pairs={{64,0},{128,64},{192,128},{256,192},{320,256},{384,320},{448,384},... | collective-permute-start | bytes 24584 | tf_op jit(solution)/shard_map/ppermute | solution.py:26
  137.8 0.1 fusion.3
  138.0 1.2 collective-permute-done.5
  139.2 11.1 %all-to-all-done.3 = bf16[64,1,8,128]{3,2,1,0:T(8,128)(2,1)S(1)} async-done(((bf16[64,1,8,128]{3,2,1,0:T(8,128)(2,1)}), bf16[64,1,8,128]{3,2,1,0:T(8,128)(2,1)S(1)}, u32[]{:S(2)}, u32[]{:S(2)}) %all-to-all-start.3) | async-done | bytes 131104 | tf_op jit(solution)/shard_map/all_to_all | solution.py:56
  150.3 0.6 gather_fusion.8
  150.9 0.2 convolution_bitcast_fusion.4
  151.0 0.1 fusion.12
  151.2 0.1 fusion.19
  151.3 0.1 fusion.21
  151.4 27.0 %all-reduce.1 = (f32[32,8]{0,1:T(8,128)S(1)}, f32[8,8]{0,1:T(8,128)S(1)}, f32[32,32]{1,0:T(8,128)S(1)}) all-reduce(f32[32,8]{0,1:T(8,128)S(1)} %fusion.21, f32[8,8]{0,1:T(8,128)S(1)} %fusion.19, f32[32,32]{1,0:T(8,128)S(1)} %fusion.3), channel_id=1, replica_groups=mesh['group_0'=8,'group_1'=2,'member_0'=16,'member_1'=4] {'group_0'}, use_global_device_ids=true, to_apply=%region_2.0 | all-reduce | flops 1344 | bytes 10752 | tf_op jit(solution)/shard_map/psum | solution.py:35
  178.4 3.4 %all-reduce.3 = (f32[32,8]{0,1:T(8,128)S(1)}, f32[8,8]{0,1:T(8,128)S(1)}, f32[32,32]{1,0:T(8,128)S(1)}) all-reduce(f32[32,8]{0,1:T(8,128)S(1)} %get-tuple-element.15, f32[8,8]{0,1:T(8,128)S(1)} %get-tuple-element.16, f32[32,32]{1,0:T(8,128)S(1)} %get-tuple-element.17), channel_id=1, replica_groups=mesh['group_0'=8,'group_1'=2,'member_0'=16,'member_1'=4] {'group_1'}, use_global_device_ids=true, to_apply=%region_3.0 | all-reduce | flops 1344 | bytes 10752 | tf_op jit(solution)/shard_map/psum | solution.py:35
  181.8 53.3 %all-reduce = (f32[32,8]{0,1:T(8,128)S(1)}, f32[8,8]{0,1:T(8,128)S(1)}, f32[32,32]{1,0:T(8,128)S(1)}) all-reduce(f32[32,8]{0,1:T(8,128)S(1)} %get-tuple-element.21, f32[8,8]{0,1:T(8,128)S(1)} %get-tuple-element.22, f32[32,32]{1,0:T(8,128)S(1)} %get-tuple-element.23), channel_id=1, replica_groups=mesh['group_0'=8,'group_1'=2,'member_0'=16,'member_1'=4] {'member_0'}, use_global_device_ids=true, to_apply=%region_4.0 | all-reduce | flops 1344 | bytes 10752 | tf_op jit(solution)/shard_map/psum | solution.py:35
  235.2 15.2 %all-reduce.2 = (f32[32,8]{0,1:T(8,128)S(1)}, f32[8,8]{0,1:T(8,128)S(1)}, bf16[32,32]{1,0:T(8,128)(2,1)S(1)}) all-reduce(f32[32,8]{0,1:T(8,128)S(1)} %get-tuple-element.12, f32[8,8]{0,1:T(8,128)S(1)} %get-tuple-element.13, ...), channel_id=1, replica_groups=mesh['group_0'=8,'group_1'=2,'member_0'=16,'member_1'=4] {'member_1'}, use_global_device_ids=true, to_apply=%region_5.0 | all-reduce | flops 1344 | bytes 8704 | tf_op jit(solution)/shard_map/psum | solution.py:35
  250.4 0.1 fusion.18
  250.5 0.3 fusion.15
  250.8 0.1 copy.30
  250.9 0.7 cholesky.17
  251.6 0.1 select_reduce_fusion
  251.6 0.6 compare_reduce_fusion
  252.3 0.6 fusion.27
  252.9 0.6 custom-call.6
  253.6 0.2 convolution_bitcast_fusion.7
  253.8 0.8 convolution_bitcast_fusion.1
  (27 shorter events, 0.2 us)
Async XLA Ops:
  0.6 98.0 %copy-start = (bf16[4096,256]{1,0:T(8,128)(2,1)S(1)}, bf16[4096,256]{1,0:T(8,128)(2,1)}, u32[]{:S(2)}) copy-start(bf16[4096,256]{1,0:T(8,128)(2,1)} %param.18) | copy-start | bytes 6291460
  0.6 98.6 %copy-start.5 = (bf16[2,128,128]{2,1,0:T(8,128)(2,1)S(1)}, bf16[2,128,128]{2,1,0:T(8,128)(2,1)}, u32[]{:S(2)}) copy-start(bf16[2,128,128]{2,1,0:T(8,128)(2,1)} %param.17) | copy-start | bytes 196612
  0.7 98.3 %copy-start.9 = (s32[2]{0:T(128)S(1)}, s32[2]{0:T(128)}, u32[]{:S(2)}) copy-start(s32[2]{0:T(128)} %param.16) | copy-start | bytes 28
  3.7 39.9 %all-to-all-start = ((bf16[64,1,8,128]{3,2,1,0:T(8,128)(2,1)}), bf16[64,1,8,128]{3,2,1,0:T(8,128)(2,1)S(1)}, u32[]{:S(2)}, u32[]{:S(2)}) async-start(bf16[64,1,8,128]{3,2,1,0:T(8,128)(2,1)} %bitcast.5), calls=%async_computation | async-start | bytes 262144 | tf_op jit(solution)/shard_map/all_to_all | solution.py:56
  27.2 6.4 %collective-permute-start = (bf16[1,4,8,128]{3,2,1,0:T(8,128)(2,1)S(1)}, bf16[1,4,8,128]{3,2,1,0:T(8,128)(2,1)S(1)}, u32[]{:S(2)}, u32[]{:S(2)}) collective-permute-start(bf16[1,4,8,128]{3,2,1,0:T(8,128)(2,1)S(1)} %bitcast.142), channel_id=1, source_target_pairs={{0,64},{64,128},{128,192},{192,256},{256,320},{320,384},{384,448},... | collective-permute-start | bytes 24584 | tf_op jit(solution)/shard_map/ppermute | solution.py:24
  29.1 5.0 %collective-permute-start.1 = (bf16[1,4,8,128]{3,2,1,0:T(8,128)(2,1)S(1)}, bf16[1,4,8,128]{3,2,1,0:T(8,128)(2,1)S(1)}, u32[]{:S(2)}, u32[]{:S(2)}) collective-permute-start(bf16[1,4,8,128]{3,2,1,0:T(8,128)(2,1)S(1)} %bitcast.143), channel_id=1, source_target_pairs={{64,0},{128,64},{192,128},{256,192},{320,256},{384,320},{448,384},... | collective-permute-start | bytes 24584 | tf_op jit(solution)/shard_map/ppermute | solution.py:26
  44.3 81.1 %copy-start.2 = (bf16[2,8,128,128]{3,2,1,0:T(8,128)(2,1)S(1)}, bf16[2,8,128,128]{3,2,1,0:T(8,128)(2,1)}, u32[]{:S(2)}) copy-start(bf16[2,8,128,128]{3,2,1,0:T(8,128)(2,1)} %param.10) | copy-start | bytes 1572868
  45.6 80.0 %copy-start.3 = (bf16[2,128,128]{2,1,0:T(8,128)(2,1)S(1)}, bf16[2,128,128]{2,1,0:T(8,128)(2,1)}, u32[]{:S(2)}) copy-start(bf16[2,128,128]{2,1,0:T(8,128)(2,1)} %param.14) | copy-start | bytes 196612
  45.6 80.0 %copy-start.4 = (bf16[2,32,128]{2,1,0:T(8,128)(2,1)S(1)}, bf16[2,32,128]{2,1,0:T(8,128)(2,1)}, u32[]{:S(2)}) copy-start(bf16[2,32,128]{2,1,0:T(8,128)(2,1)} %param.19) | copy-start | bytes 49156
  45.6 80.0 %copy-start.6 = (bf16[2,128,128]{2,1,0:T(8,128)(2,1)S(1)}, bf16[2,128,128]{2,1,0:T(8,128)(2,1)}, u32[]{:S(2)}) copy-start(bf16[2,128,128]{2,1,0:T(8,128)(2,1)} %param.15) | copy-start | bytes 196612
  100.6 24.1 %all-to-all-start.2 = ((bf16[64,1,8,128]{3,2,1,0:T(8,128)(2,1)}), bf16[64,1,8,128]{3,2,1,0:T(8,128)(2,1)S(1)}, u32[]{:S(2)}, u32[]{:S(2)}) async-start(bf16[64,1,8,128]{3,2,1,0:T(8,128)(2,1)} %bitcast.20), calls=%async_computation.2 | async-start | bytes 262144 | tf_op jit(solution)/shard_map/all_to_all | solution.py:56
  107.3 5.6 %collective-permute-start.2 = (bf16[1,4,8,128]{3,2,1,0:T(8,128)(2,1)S(1)}, bf16[1,4,8,128]{3,2,1,0:T(8,128)(2,1)S(1)}, u32[]{:S(2)}, u32[]{:S(2)}) collective-permute-start(bf16[1,4,8,128]{3,2,1,0:T(8,128)(2,1)S(1)} %bitcast.146), channel_id=1, source_target_pairs={{0,64},{64,128},{128,192},{192,256},{256,320},{320,384},{384,448},... | collective-permute-start | bytes 24584 | tf_op jit(solution)/shard_map/ppermute | solution.py:24
  109.2 5.0 %collective-permute-start.3 = (bf16[1,4,8,128]{3,2,1,0:T(8,128)(2,1)S(1)}, bf16[1,4,8,128]{3,2,1,0:T(8,128)(2,1)S(1)}, u32[]{:S(2)}, u32[]{:S(2)}) collective-permute-start(bf16[1,4,8,128]{3,2,1,0:T(8,128)(2,1)S(1)} %bitcast.147), channel_id=1, source_target_pairs={{64,0},{128,64},{192,128},{256,192},{320,256},{384,320},{448,384},... | collective-permute-start | bytes 24584 | tf_op jit(solution)/shard_map/ppermute | solution.py:26
  125.8 128.8 %copy-start.1 = (bf16[2,8,128]{2,1,0:T(8,128)(2,1)}, bf16[2,8,128]{2,1,0:T(8,128)(2,1)S(1)}, u32[]{:S(2)}) copy-start(bf16[2,8,128]{2,1,0:T(8,128)(2,1)S(1)} %fusion.11) | copy-start | bytes 12292
  127.1 23.2 %all-to-all-start.3 = ((bf16[64,1,8,128]{3,2,1,0:T(8,128)(2,1)}), bf16[64,1,8,128]{3,2,1,0:T(8,128)(2,1)S(1)}, u32[]{:S(2)}, u32[]{:S(2)}) async-start(bf16[64,1,8,128]{3,2,1,0:T(8,128)(2,1)} %bitcast.29), calls=%async_computation.3 | async-start | bytes 262144 | tf_op jit(solution)/shard_map/all_to_all | solution.py:56
  132.3 5.7 %collective-permute-start.4 = (bf16[1,4,8,128]{3,2,1,0:T(8,128)(2,1)S(1)}, bf16[1,4,8,128]{3,2,1,0:T(8,128)(2,1)S(1)}, u32[]{:S(2)}, u32[]{:S(2)}) collective-permute-start(bf16[1,4,8,128]{3,2,1,0:T(8,128)(2,1)S(1)} %bitcast.144), channel_id=1, source_target_pairs={{0,64},{64,128},{128,192},{192,256},{256,320},{320,384},{384,448},... | collective-permute-start | bytes 24584 | tf_op jit(solution)/shard_map/ppermute | solution.py:24
  134.6 4.6 %collective-permute-start.5 = (bf16[1,4,8,128]{3,2,1,0:T(8,128)(2,1)S(1)}, bf16[1,4,8,128]{3,2,1,0:T(8,128)(2,1)S(1)}, u32[]{:S(2)}, u32[]{:S(2)}) collective-permute-start(bf16[1,4,8,128]{3,2,1,0:T(8,128)(2,1)S(1)} %bitcast.145), channel_id=1, source_target_pairs={{64,0},{128,64},{192,128},{256,192},{320,256},{384,320},{448,384},... | collective-permute-start | bytes 24584 | tf_op jit(solution)/shard_map/ppermute | solution.py:26
  250.4 4.2 %copy-start.7 = (f32[32,8]{0,1:T(8,128)}, f32[32,8]{0,1:T(8,128)S(1)}, u32[]{:S(2)}) copy-start(f32[32,8]{0,1:T(8,128)S(1)} %get-tuple-element.18) | copy-start | bytes 3076
  250.9 3.7 %copy-start.8 = (f32[8,8]{1,0:T(8,128)}, f32[8,8]{1,0:T(8,128)S(1)}, u32[]{:S(2)}) copy-start(f32[8,8]{1,0:T(8,128)S(1)} %copy.30) | copy-start | bytes 772
where the time goes:
time: 255 us
  blocking collectives  150 us (59%)
  starting transfers between devices  49.6 us (19%)
  waiting for transfers between devices  34.3 us (13%)
  matrix products  7.46 us (3%)
  local copies, waits for them, and re-layouts  7.44 us (3%)
  other arithmetic  4.95 us (2%)
    psum x6, blocking collectives, over_axes(): shard = lax.psum(shard, axis)  136 us
    all_to_all x3, starting transfers between devices, extend_tiles(): lax.all_to_all(outgoing, MEMBER, split_axis=0, concat_axis=0, tiled=True)  32.9 us
    all_to_all x3, waiting for transfers between devices, extend_tiles(): lax.all_to_all(outgoing, MEMBER, split_axis=0, concat_axis=0, tiled=True)  31.2 us
    all_to_all x1, blocking collectives, from_everyone(): return lax.all_to_all(copies, axis, split_axis=0, concat_axis=0, tiled=True)  13.9 us
    ppermute x3, starting transfers between devices, extended_2(): lax.ppermute(head, axis, [((i + 1) % count, i) for i in range(ends)])  10.5 us
    ppermute x3, starting transfers between devices, extended_2(): lax.ppermute(tail, axis, [(i, (i + 1) % count) for i in range(ends)])  6.19 us
  transfers between devices with their start and end apart: 9, of which 6 were waited for; matrix products, arithmetic and copies ran while one was open for 1% of the time, Pallas kernels for 0%

commit v1 on v0

v1 whole, which is shorter than its diff:
```python
import functools

import jax
import jax.numpy as jnp
from jax import lax
from jax.experimental import pallas as pl
from jax.experimental.pallas import tpu as pltpu
from jax.sharding import PartitionSpec as P

TILE = 128
NVEC = 8
NB = 32
CTG = 2
TD = 2
K = 8
GG = 4
NX = 4
F32 = jnp.float32
BF16 = jnp.bfloat16
HIGHEST = lax.Precision.HIGHEST
MESH = pl.DeviceIdType.MESH
NT_DIMS = (((1,), (1,)), ((), ()))


def dot(left, right):
    return jnp.dot(left, right, preferred_element_type=F32)


def dot_nt(left, right):
    return lax.dot_general(left, right, NT_DIMS, preferred_element_type=F32)


def exact(left, right):
    return jnp.dot(left, right, preferred_element_type=F32, precision=HIGHEST)


def exact_nt(left, right):
    return lax.dot_general(left, right, NT_DIMS, preferred_element_type=F32, precision=HIGHEST)


def cycle(
    groups, members, rows_all,
    off_cols, member_send, group_send, agg_map,
    off_hbm, diag_hbm, smooth_hbm, prolong_hbm, inv_hbm, basis_hbm,
    prec_ref, coef_ref, gram_ref, new_ref,
    off, diag, smooth, prolong, inv, basis,
    vals, out_tiles, out_rim, turn_0, turn_1, turn_2, ext_0, ext_1, ext_2,
    cx, cz, cg, corr,
    bz, bx, bg, fg, fx, fz,
    c_own, s_own, g_own, b_own, b2_own, b3_own, f_own, f2_own, f3_own,
    load_sem, turn_send, turn_recv, ex_send, ex_recv, st_send, st_recv,
):
    nz = members // NX
    ext = (ext_0, ext_1, ext_2)
    turn = (turn_0, turn_1, turn_2)
    g = lax.axis_index("group")
    m = lax.axis_index("member")
    z = lax.div(m, NX)
    x = lax.rem(m, NX)
    scale_rows = 1.0 / rows_all

    def at_member(pz, px):
        return {"group": g, "member": pz * NX + px}

    xs = [lax.rem(x + d, NX) for d in range(NX)]

    def z_of(k):
        return lax.rem(z + nz // 2 + lax.div(k + 1, 2) * (1 - 2 * lax.rem(k, 2)), nz)

    def each_z(act):
        def step(k, carry):
            act(z_of(k))
            return carry

        lax.fori_loop(0, nz - 1, step, 0)

    def each_group(act):
        def step(k, carry):
            act(lax.rem(g + 1 + k, groups))
            return carry

        lax.fori_loop(0, groups - 1, step, 0)

    barrier = pltpu.get_barrier_semaphore()
    each_z(
        lambda pz: pl.semaphore_signal(
            barrier, inc=1, device_id=at_member(pz, x), device_id_type=MESH
        )
    )
    for d in range(1, NX):
        pl.semaphore_signal(barrier, inc=1, device_id=at_member(z, xs[d]), device_id_type=MESH)
    each_group(
        lambda pg: pl.semaphore_signal(
            barrier, inc=1, device_id={"group": pg, "member": m}, device_id_type=MESH
        )
    )

    loads = [
        pltpu.make_async_copy(src, dst, load_sem.at[i])
        for i, (src, dst) in enumerate(
            (
                (basis_hbm, basis),
                (smooth_hbm, smooth),
                (off_hbm, off),
                (diag_hbm, diag),
                (prolong_hbm, prolong),
                (inv_hbm, inv),
            )
        )
    ]
    for load in loads:
        load.start()

    loads[0].wait()
    loads[1].wait()
    last = [basis[t, NB - NVEC :, :] for t in range(TD)]
    first = [dot(last[t], smooth[t]).astype(BF16) for t in range(TD)]

    def fill(r, tiles):
        for t in range(TD):
            vals[r, t] = tiles[t]
            ext[r][t] = tiles[t]

        def step(pz, carry):
            for px in range(NX):
                out_tiles[r, px, pz] = vals[r, member_send[pz * NX + px]]
            turn[r][x, pz] = vals[r, member_send[pz * NX + x]]
            return carry

        lax.fori_loop(0, nz, step, 0, unroll=True)
        for s in range(GG):
            out_rim[r, s] = vals[r, group_send[s]]

    def send_tiles(r):
        for d in (2, 1, 3) if NX == 4 else range(1, NX):
            pltpu.make_async_remote_copy(
                src_ref=out_tiles.at[r, xs[d]],
                dst_ref=turn[r].at[x],
                send_sem=turn_send.at[r],
                recv_sem=turn_recv.at[r],
                device_id=at_member(z, xs[d]),
                device_id_type=MESH,
            ).start()
        for step, base in ((1, TD + members), (groups - 1, TD + members + GG)):
            pltpu.make_async_remote_copy(
                src_ref=out_rim.at[r],
                dst_ref=ext[r].at[pl.ds(base, GG)],
                send_sem=ex_send.at[r],
                recv_sem=ex_recv.at[r],
                device_id={"group": lax.rem(g + step, groups), "member": m},
                device_id_type=MESH,
            ).start()

    moved = members - NX + 2 * GG

    def take_tiles(r):
        view = turn[r].at[pl.ds(0, NX - 1)]
        pltpu.make_async_copy(view, view, turn_recv.at[r]).wait()

        def act(pz):
            pltpu.make_async_remote_copy(
                src_ref=turn[r].at[:, pz],
                dst_ref=ext[r].at[pl.ds(TD + z * NX, NX)],
                send_sem=ex_send.at[r],
                recv_sem=ex_recv.at[r],
                device_id=at_member(pz, x),
                device_id_type=MESH,
            ).start()

        each_z(act)
        for px in range(NX):
            ext[r][TD + z * NX + px] = turn[r][px, z]
        view = ext[r].at[pl.ds(0, moved)]
        pltpu.make_async_copy(view, view, ex_recv.at[r]).wait()

        @pl.when(g == 0)
        def _():
            ext[r][TD + members : TD + members + GG] = jnp.zeros((GG, NVEC, TILE), BF16)

        @pl.when(g == groups - 1)
        def _():
            ext[r][TD + members + GG : TD + members + 2 * GG] = jnp.zeros((GG, NVEC, TILE), BF16)

    def operate(r, tiles):
        result = []
        for t in range(TD):
            picked = jnp.concatenate([ext[r][off_cols[t, k]] for k in range(K)], axis=1)
            result.append(dot(tiles[t], diag[t]) + dot(picked, off[t]))
        return result

    def push(i, src, dst, device):
        pltpu.make_async_remote_copy(
            src_ref=src,
            dst_ref=dst,
            send_sem=st_send.at[i],
            recv_sem=st_recv.at[i],
            device_id=device,
            device_id_type=MESH,
        ).start()

    def take(i, buf, count):
        view = buf.at[pl.ds(0, count)]
        pltpu.make_async_copy(view, view, st_recv.at[i]).wait()

    def send_x(i, own, buf):
        for d in range(1, NX):
            push(i, own, buf.at[x], at_member(z, xs[d]))

    def send_z(i, own, buf):
        def step(k, carry):
            push(i, own, buf.at[z], at_member(z_of(k), x))
            return carry

        lax.fori_loop(0, nz - 1, step, 0)

    def send_g(i, own, buf):
        each_group(lambda pg: push(i, own, buf.at[g], {"group": pg, "member": m}))

    def total(buf, count):
        result = buf[0]
        for j in range(1, count):
            result = result + buf[j]
        return result

    fill(0, first)

    lanes = lax.broadcasted_iota(jnp.int32, (NVEC, TILE), 1)
    packed = jnp.zeros((NVEC, TILE), F32)
    for a in range(NB // NVEC):
        rows = jnp.zeros((NVEC, TILE), F32)
        for t in range(TD):
            whole = basis[t]
            four = jnp.concatenate([whole] * (TILE // NB), axis=0)
            rows = rows + dot_nt(basis[t, NVEC * a : NVEC * (a + 1), :], four)
        packed = jnp.where(lax.div(lanes, NB) == a, rows, packed)
    packed = packed * scale_rows
    b_own[...] = packed
    bz[z] = packed
    for load in loads[2:]:
        load.wait()

    pl.semaphore_wait(barrier, nz + NX + groups - 3)
    send_tiles(0)
    take_tiles(0)

    pieces = []
    applied = operate(0, first)
    for t in range(TD):
        residual = (last[t].astype(F32) - applied[t]).astype(BF16)
        pieces.append(dot_nt(residual, prolong[t]))
    part = []
    for a in range(CTG):
        part.append(
            sum(jnp.where(agg_map[t] == a, pieces[t], jnp.zeros_like(pieces[t])) for t in range(TD))
        )
    part = jnp.concatenate(part, axis=0)
    c_own[...] = part
    cx[x] = part
    send_x(0, c_own, cx)
    send_z(3, b_own, bz)
    take(0, cx, NX - 1)
    part = total(cx, NX)
    s_own[...] = part
    cz[z] = part
    send_z(1, s_own, cz)

    take(3, bz, nz - 1)
    part = total(bz, nz)
    b2_own[...] = part
    bx[x] = part
    send_x(4, b2_own, bx)

    take(1, cz, nz - 1)
    part = total(cz, nz).astype(BF16)
    for a in range(CTG):
        g_own[a] = part[NVEC * a : NVEC * (a + 1), :]
        cg[g, a] = part[NVEC * a : NVEC * (a + 1), :]
    send_g(2, g_own, cg)

    take(4, bx, NX - 1)
    part = total(bx, NX)
    b3_own[...] = part
    bg[g] = part

    take(2, cg, groups - 1)
    coarse = jnp.concatenate([cg[c // CTG, c % CTG] for c in range(groups * CTG)], axis=1)
    correction = dot(coarse, inv[...]).astype(BF16)
    for a in range(CTG):
        corr[a] = correction[:, TILE * a : TILE * (a + 1)]
    second = []
    for t in range(TD):
        second.append((first[t].astype(F32) + dot(corr[agg_map[t]], prolong[t])).astype(BF16))
    fill(1, second)
    send_tiles(1)
    send_g(5, b3_own, bg)
    take_tiles(1)

    applied = operate(1, second)
    precond = []
    for t in range(TD):
        residual = (last[t].astype(F32) - applied[t]).astype(BF16)
        precond.append((second[t].astype(F32) + dot(residual, smooth[t])).astype(BF16))
    fill(2, precond)
    send_tiles(2)
    for t in range(TD):
        prec_ref[t] = precond[t]

    take(5, bg, groups - 1)
    packed = total(bg, groups)
    basis_total = jnp.concatenate(
        [
            packed if a == 0 else pltpu.roll(packed, TILE - NB * a, 1)
            for a in range(NB // NVEC)
        ],
        axis=0,
    )
    wide_lanes = lax.broadcasted_iota(jnp.int32, (NB, TILE), 1)
    basis_total = jnp.where(wide_lanes < NB, basis_total, 0.0)
    take_tiles(2)

    applied = [value.astype(BF16) for value in operate(2, precond)]
    part = jnp.zeros((NVEC, TILE), F32)
    for t in range(TD):
        right = jnp.concatenate(
            [basis[t], applied[t], jnp.zeros((TILE - NB - NVEC, TILE), BF16)], axis=0
        )
        part = part + dot_nt(applied[t], right)
    part = part * scale_rows
    f_own[...] = part
    fg[g] = part
    send_g(6, f_own, fg)
    take(6, fg, groups - 1)
    part = total(fg, groups)
    f2_own[...] = part
    fx[x] = part
    send_x(7, f2_own, fx)
    take(7, fx, NX - 1)
    part = total(fx, NX)
    f3_own[...] = part
    fz[z] = part
    send_z(8, f3_own, fz)
    take(8, fz, nz - 1)
    part = total(fz, nz)

    coef = jnp.where(lanes < NB, part, 0.0)
    square = pltpu.roll(part, TILE - NB, 1)
    coef_ref[...] = jnp.transpose(coef)[:NB, :]
    narrow = coef[:, :NB]
    through = exact(narrow, basis_total)
    gram = square[:, :NVEC] - 2.0 * exact_nt(coef, coef) + exact_nt(through, coef)
    gram_ref[...] = gram
    rest = [applied[t].astype(F32) - exact(narrow, basis[t].astype(F32)) for t in range(TD)]
    ids = lax.broadcasted_iota(jnp.int32, (NVEC, 1), 0)
    left = gram
    for j in range(NVEC - 1):
        pivot_row = left[j : j + 1, :]
        factor = left[:, j : j + 1] / left[j : j + 1, j : j + 1]
        factor = jnp.where(ids > j, factor, 0.0)
        left = left - factor * pivot_row
        rest = [r - factor * r[j : j + 1, :] for r in rest]
    row_ids = lax.broadcasted_iota(jnp.int32, (NVEC, NVEC), 0)
    col_ids = lax.broadcasted_iota(jnp.int32, (NVEC, NVEC), 1)
    pivots = jnp.sum(jnp.where(row_ids == col_ids, left, 0.0), axis=1, keepdims=True)
    gain = 1.0 / jnp.sqrt(pivots)
    for t in range(TD):
        new_ref[t] = rest[t] * gain

    for r in range(3):
        view = ext[r].at[pl.ds(0, moved)]
        pltpu.make_async_copy(view, view, ex_send.at[r]).wait()
        view = turn[r].at[pl.ds(0, NX - 1)]
        pltpu.make_async_copy(view, view, turn_send.at[r]).wait()
    for i, (buf, count) in enumerate(
        (
            (cx, NX), (cz, nz), (cg, groups), (bz, nz), (bx, NX), (bg, groups),
            (fg, groups), (fx, NX), (fz, nz),
        )
    ):
        view = buf.at[pl.ds(0, count - 1)]
        pltpu.make_async_copy(view, view, st_send.at[i]).wait()


def local(groups, members, off_tiles, off_cols, member_send, group_send, diag_tiles, smoother,
          agg_map, prolong, coarse_inv, krylov_basis):
    nz = members // NX
    rows_all = TD * TILE * members * groups
    hbm = pl.BlockSpec(memory_space=pl.ANY)
    smem = pl.BlockSpec(memory_space=pltpu.SMEM)
    vmem = pl.BlockSpec(memory_space=pltpu.VMEM)
    slots = TD + members + 2 * GG
    wide = (NVEC, TILE)
    call = pl.pallas_call(
        functools.partial(cycle, groups, members, rows_all),
        out_shape=(
            jax.ShapeDtypeStruct((TD, NVEC, TILE), BF16),
            jax.ShapeDtypeStruct((NB, NVEC), F32),
            jax.ShapeDtypeStruct((NVEC, NVEC), F32),
            jax.ShapeDtypeStruct((TD, NVEC, TILE), F32),
        ),
        in_specs=[smem] * 4 + [hbm] * 6,
        out_specs=(vmem,) * 4,
        scratch_shapes=[
            pltpu.VMEM((TD, K * TILE, TILE), BF16),
            pltpu.VMEM((TD, TILE, TILE), BF16),
            pltpu.VMEM((TD, TILE, TILE), BF16),
            pltpu.VMEM((TD, TILE, TILE), BF16),
            pltpu.VMEM((groups * CTG * TILE, CTG * TILE), BF16),
            pltpu.VMEM((TD, NB, TILE), BF16),
            pltpu.VMEM((3, TD, NVEC, TILE), BF16),
            pltpu.VMEM((3, NX, nz, NVEC, TILE), BF16),
            pltpu.VMEM((3, GG, NVEC, TILE), BF16),
            pltpu.VMEM((NX, nz, NVEC, TILE), BF16),
            pltpu.VMEM((NX, nz, NVEC, TILE), BF16),
            pltpu.VMEM((NX, nz, NVEC, TILE), BF16),
            pltpu.VMEM((slots, NVEC, TILE), BF16),
            pltpu.VMEM((slots, NVEC, TILE), BF16),
            pltpu.VMEM((slots, NVEC, TILE), BF16),
            pltpu.VMEM((NX, CTG * NVEC, TILE), F32),
            pltpu.VMEM((nz, CTG * NVEC, TILE), F32),
            pltpu.VMEM((groups, CTG, NVEC, TILE), BF16),
            pltpu.VMEM((CTG, NVEC, TILE), BF16),
            pltpu.VMEM((nz, *wide), F32),
            pltpu.VMEM((NX, *wide), F32),
            pltpu.VMEM((groups, *wide), F32),
            pltpu.VMEM((groups, *wide), F32),
            pltpu.VMEM((NX, *wide), F32),
            pltpu.VMEM((nz, *wide), F32),
            pltpu.VMEM((CTG * NVEC, TILE), F32),
            pltpu.VMEM((CTG * NVEC, TILE), F32),
            pltpu.VMEM((CTG, NVEC, TILE), BF16),
            pltpu.VMEM(wide, F32),
            pltpu.VMEM(wide, F32),
            pltpu.VMEM(wide, F32),
            pltpu.VMEM(wide, F32),
            pltpu.VMEM(wide, F32),
            pltpu.VMEM(wide, F32),
            pltpu.SemaphoreType.DMA((6,)),
            pltpu.SemaphoreType.DMA((3,)),
            pltpu.SemaphoreType.DMA((3,)),
            pltpu.SemaphoreType.DMA((3,)),
            pltpu.SemaphoreType.DMA((3,)),
            pltpu.SemaphoreType.DMA((9,)),
            pltpu.SemaphoreType.DMA((9,)),
        ],
        compiler_params=pltpu.CompilerParams(collective_id=0, has_side_effects=True),
        name="cycle",
    )
    return call(
        off_cols,
        member_send.reshape(members),
        group_send.reshape(GG),
        agg_map,
        off_tiles.reshape(TD, K * TILE, TILE),
        diag_tiles,
        smoother,
        prolong,
        coarse_inv,
        krylov_basis,
    )


def solution(mesh):
    groups, members = mesh.shape["group"], mesh.shape["member"]
    both = ("group", "member")
    in_specs = (
        P(both, None, None, None),
        P(both, None),
        P(both, None, None),
        P(both, None),
        P(both, None, None),
        P(both, None, None),
        P(both),
        P(both, None, None),
        P(None, "group"),
        P(both, None, None),
    )
    out_specs = (P(both, None, None), P(), P(), P(both, None, None))
    return jax.shard_map(
        functools.partial(local, groups, members),
        mesh=mesh,
        in_specs=in_specs,
        out_specs=out_specs,
        check_vma=False,
    )
```

time: 255 us -> 101 us (0.40)
  blocking collectives: 150 us -> 0 us
  Pallas kernels: 0 us -> 94.4 us
  starting transfers between devices: 49.6 us -> 0 us
  waiting for transfers between devices: 34.3 us -> 0 us
  matrix products: 7.46 us -> 0 us
  other arithmetic: 4.95 us -> 0 us
    psum x6 -> x0, blocking collectives: 136 us -> none  [over_axes(): shard = lax.psum(shard, axis)]
    pallas_call x0 -> x1, Pallas kernels: none -> 94.4 us  [local(): call(off_cols, member_send.reshape(members), group_send.reshape(GG), agg_...]
    all_to_all x3 -> x0, starting transfers between devices: 32.9 us -> none  [extend_tiles(): lax.all_to_all(outgoing, MEMBER, split_axis=0, concat_axis=0, tiled=True)]
    all_to_all x3 -> x0, waiting for transfers between devices: 31.2 us -> none  [extend_tiles(): lax.all_to_all(outgoing, MEMBER, split_axis=0, concat_axis=0, tiled=True)]
    ppermute x6 -> x0, starting transfers between devices: 16.7 us -> none  [the longest x3 10.5 us: extended_2(): lax.ppermute(head, axis, [((i + 1) % count, i) for i in range(ends)])]
    all_to_all x1 -> x0, blocking collectives: 13.9 us -> none  [from_everyone(): return lax.all_to_all(copies, axis, split_axis=0, concat_axis=0, tiled=True)]
    dot_general x17 -> x0, matrix products: 7.27 us -> none  [the longest x4 2.07 us: exact_product(): return jnp.einsum(form, first_operand, second_operand)]
    gather x9 -> x0, local copies, waits for them, and re-layouts: 7.22 us -> none  [the longest x3 3.82 us: extend_tiles(): values[member_send[0].reshape(-1)].reshape(members, GH, NVEC, TILE)]
  transfers between devices with their start and end apart: 9 -> 0, of which waited for: 6 -> 0; matrix products, arithmetic and copies ran while one was open for 1% -> 0% of each run, Pallas kernels for 0% -> 0%
where the time goes in v1:
time: 101 us; the launch traced here: 100 us
  Pallas kernels  94.4 us (93%)
  local copies, waits for them, and re-layouts  5.21 us (5%)
    pallas_call x1, Pallas kernels, local(): call(off_cols, member_send.reshape(members), group_send.reshape(GG), agg_...  94.4 us
    unnamed x3, local copies, waits for them, and re-layouts  3.83 us

profile of v1, /device:TPU:8, one launch (start us, length us, event | category | flops | bytes accessed | tf_op | source)
XLA Modules:
  0.0 100.2 jit_solution(18125424068761640488)
XLA Ops:
  0.6 94.4 %cycle.1 = (bf16[2,8,128]{2,1,0:T(8,128)(2,1)}, f32[32,8]{1,0:T(8,128)}, f32[8,8]{1,0:T(8,128)}, f32[2,8,128]{2,1,0:T(8,128)}) custom-call(s32[2,8]{1,0:T(2,128)} %off_cols.1, s32[64]{0:T(128)} %bitcast.4, s32[4]{0:T(128)} %bitcast.5, s32[2]{0:T(128)} %agg_map.1, bf16[2,1024,128]{2,1,0:T(8,128)(2,1)} %bitcast.3, bf16[2,128,128]{2,1,0:T(8,128)(2,1)} %diag_hbm.1, ...), custom_call_target="tpu_custom_call" | custom-call | tf_op jit(solution)/shard_map/cycle/pallas_call | solution.py:448
  95.0 1.4 %copy.14 = f32[32,8]{0,1:T(8,128)} copy(f32[32,8]{1,0:T(8,128)} %get-tuple-element.5) | data formatting | bytes 2048 | tf_op jit(solution)/shard_map/cycle/pallas_call | solution.py:448
  96.4 1.3 %copy.18 = bf16[2,8,128]{2,1,0:T(8,128)(2,1)} copy(bf16[2,8,128]{2,1,0:T(8,128)(2,1)} %get-tuple-element.12) | data formatting | bytes 8192
  97.7 1.3 %copy.19 = f32[8,8]{1,0:T(8,128)} copy(f32[8,8]{1,0:T(8,128)} %get-tuple-element.14) | data formatting | bytes 512
  98.9 1.3 %copy.20 = f32[2,8,128]{2,1,0:T(8,128)} copy(f32[2,8,128]{2,1,0:T(8,128)} %get-tuple-element.15) | data formatting | bytes 16384

commit v2 on v1

--- a/solution.py
+++ b/solution.py
@@ -40,9 +40,10 @@
 
 def cycle(
     groups, members, rows_all,
-    off_cols, member_send, group_send, agg_map,
+    cols_hbm, member_hbm, rim_hbm, agg_hbm,
     off_hbm, diag_hbm, smooth_hbm, prolong_hbm, inv_hbm, basis_hbm,
     prec_ref, coef_ref, gram_ref, new_ref,
+    off_cols, member_send, group_send, agg_map,
     off, diag, smooth, prolong, inv, basis,
     vals, out_tiles, out_rim, turn_0, turn_1, turn_2, ext_0, ext_1, ext_2,
     cx, cz, cg, corr,
@@ -63,6 +64,7 @@
         return {"group": g, "member": pz * NX + px}
 
     xs = [lax.rem(x + d, NX) for d in range(NX)]
+    x_order = sorted(range(1, NX), key=lambda d: -min(d, NX - d))
 
     def z_of(k):
         return lax.rem(z + nz // 2 + lax.div(k + 1, 2) * (1 - 2 * lax.rem(k, 2)), nz)
@@ -76,7 +78,8 @@
 
     def each_group(act):
         def step(k, carry):
-            act(lax.rem(g + 1 + k, groups))
+            away = lax.div(k + 1, 2) * (1 - 2 * lax.rem(k, 2))
+            act(lax.rem(g + groups // 2 + away, groups))
             return carry
 
         lax.fori_loop(0, groups - 1, step, 0)
@@ -105,11 +108,15 @@
                 (diag_hbm, diag),
                 (prolong_hbm, prolong),
                 (inv_hbm, inv),
+                (member_hbm, member_send),
+                (rim_hbm, group_send),
+                (cols_hbm, off_cols),
+                (agg_hbm, agg_map),
             )
         )
     ]
-    for load in loads:
-        load.start()
+    for i in (0, 1, 6, 7, 2, 3, 8, 9, 4, 5):
+        loads[i].start()
 
     loads[0].wait()
     loads[1].wait()
@@ -132,7 +139,7 @@
             out_rim[r, s] = vals[r, group_send[s]]
 
     def send_tiles(r):
-        for d in (2, 1, 3) if NX == 4 else range(1, NX):
+        for d in x_order:
             pltpu.make_async_remote_copy(
                 src_ref=out_tiles.at[r, xs[d]],
                 dst_ref=turn[r].at[x],
@@ -203,7 +210,7 @@
         pltpu.make_async_copy(view, view, st_recv.at[i]).wait()
 
     def send_x(i, own, buf):
-        for d in range(1, NX):
+        for d in x_order:
             push(i, own, buf.at[x], at_member(z, xs[d]))
 
     def send_z(i, own, buf):
@@ -222,6 +229,8 @@
             result = result + buf[j]
         return result
 
+    loads[6].wait()
+    loads[7].wait()
     fill(0, first)
 
     lanes = lax.broadcasted_iota(jnp.int32, (NVEC, TILE), 1)
@@ -236,8 +245,8 @@
     packed = packed * scale_rows
     b_own[...] = packed
     bz[z] = packed
-    for load in loads[2:]:
-        load.wait()
+    for i in (2, 3, 4, 5, 8, 9):
+        loads[i].wait()
 
     pl.semaphore_wait(barrier, nz + NX + groups - 3)
     send_tiles(0)
@@ -257,18 +266,11 @@
     c_own[...] = part
     cx[x] = part
     send_x(0, c_own, cx)
-    send_z(3, b_own, bz)
     take(0, cx, NX - 1)
     part = total(cx, NX)
     s_own[...] = part
     cz[z] = part
     send_z(1, s_own, cz)
-
-    take(3, bz, nz - 1)
-    part = total(bz, nz)
-    b2_own[...] = part
-    bx[x] = part
-    send_x(4, b2_own, bx)
 
     take(1, cz, nz - 1)
     part = total(cz, nz).astype(BF16)
@@ -276,11 +278,7 @@
         g_own[a] = part[NVEC * a : NVEC * (a + 1), :]
         cg[g, a] = part[NVEC * a : NVEC * (a + 1), :]
     send_g(2, g_own, cg)
-
-    take(4, bx, NX - 1)
-    part = total(bx, NX)
-    b3_own[...] = part
-    bg[g] = part
+    send_z(3, b_own, bz)
 
     take(2, cg, groups - 1)
     coarse = jnp.concatenate([cg[c // CTG, c % CTG] for c in range(groups * CTG)], axis=1)
@@ -292,7 +290,11 @@
         second.append((first[t].astype(F32) + dot(corr[agg_map[t]], prolong[t])).astype(BF16))
     fill(1, second)
     send_tiles(1)
-    send_g(5, b3_own, bg)
+    take(3, bz, nz - 1)
+    part = total(bz, nz)
+    b2_own[...] = part
+    bx[x] = part
+    send_x(4, b2_own, bx)
     take_tiles(1)
 
     applied = operate(1, second)
@@ -305,17 +307,11 @@
     for t in range(TD):
         prec_ref[t] = precond[t]
 
-    take(5, bg, groups - 1)
-    packed = total(bg, groups)
-    basis_total = jnp.concatenate(
-        [
-            packed if a == 0 else pltpu.roll(packed, TILE - NB * a, 1)
-            for a in range(NB // NVEC)
-        ],
-        axis=0,
-    )
-    wide_lanes = lax.broadcasted_iota(jnp.int32, (NB, TILE), 1)
-    basis_total = jnp.where(wide_lanes < NB, basis_total, 0.0)
+    take(4, bx, NX - 1)
+    part = total(bx, NX)
+    b3_own[...] = part
+    bg[g] = part
+    send_g(5, b3_own, bg)
     take_tiles(2)
 
     applied = [value.astype(BF16) for value in operate(2, precond)]
@@ -339,15 +335,27 @@
     f3_own[...] = part
     fz[z] = part
     send_z(8, f3_own, fz)
+    take(5, bg, groups - 1)
+    packed = total(bg, groups)
+    basis_total = jnp.concatenate(
+        [
+            packed if a == 0 else pltpu.roll(packed, TILE - NB * a, 1)
+            for a in range(NB // NVEC)
+        ],
+        axis=0,
+    )
+    wide_lanes = lax.broadcasted_iota(jnp.int32, (NB, TILE), 1)
+    wide_rows = lax.broadcasted_iota(jnp.int32, (NB, TILE), 0)
+    basis_total = jnp.where(wide_lanes < NB, basis_total, 0.0)
+    mirror = jnp.where(wide_rows == wide_lanes, 2.0, 0.0) - basis_total
     take(8, fz, nz - 1)
     part = total(fz, nz)
 
     coef = jnp.where(lanes < NB, part, 0.0)
     square = pltpu.roll(part, TILE - NB, 1)
-    coef_ref[...] = jnp.transpose(coef)[:NB, :]
+    coef_ref[...] = part[:, :NB]
     narrow = coef[:, :NB]
-    through = exact(narrow, basis_total)
-    gram = square[:, :NVEC] - 2.0 * exact_nt(coef, coef) + exact_nt(through, coef)
+    gram = square[:, :NVEC] - exact_nt(exact(narrow, mirror), coef)
     gram_ref[...] = gram
     rest = [applied[t].astype(F32) - exact(narrow, basis[t].astype(F32)) for t in range(TD)]
     ids = lax.broadcasted_iota(jnp.int32, (NVEC, 1), 0)
@@ -380,12 +388,20 @@
         pltpu.make_async_copy(view, view, st_send.at[i]).wait()
 
 
+def finish(*refs):
+    sem = refs[8]
+    copies = [pltpu.make_async_copy(refs[i], refs[4 + i], sem.at[i]) for i in range(4)]
+    for copy in copies:
+        copy.start()
+    for copy in copies:
+        copy.wait()
+
+
 def local(groups, members, off_tiles, off_cols, member_send, group_send, diag_tiles, smoother,
           agg_map, prolong, coarse_inv, krylov_basis):
     nz = members // NX
     rows_all = TD * TILE * members * groups
-    hbm = pl.BlockSpec(memory_space=pl.ANY)
-    smem = pl.BlockSpec(memory_space=pltpu.SMEM)
+    hbm = pl.BlockSpec(memory_space=pltpu.HBM)
     vmem = pl.BlockSpec(memory_space=pltpu.VMEM)
     slots = TD + members + 2 * GG
     wide = (NVEC, TILE)
@@ -393,13 +409,17 @@
         functools.partial(cycle, groups, members, rows_all),
         out_shape=(
             jax.ShapeDtypeStruct((TD, NVEC, TILE), BF16),
-            jax.ShapeDtypeStruct((NB, NVEC), F32),
+            jax.ShapeDtypeStruct((NVEC, NB), F32),
             jax.ShapeDtypeStruct((NVEC, NVEC), F32),
             jax.ShapeDtypeStruct((TD, NVEC, TILE), F32),
         ),
-        in_specs=[smem] * 4 + [hbm] * 6,
+        in_specs=[hbm] * 10,
         out_specs=(vmem,) * 4,
         scratch_shapes=[
+            pltpu.SMEM((TD, K), jnp.int32),
+            pltpu.SMEM((members,), jnp.int32),
+            pltpu.SMEM((GG,), jnp.int32),
+            pltpu.SMEM((TD,), jnp.int32),
             pltpu.VMEM((TD, K * TILE, TILE), BF16),
             pltpu.VMEM((TD, TILE, TILE), BF16),
             pltpu.VMEM((TD, TILE, TILE), BF16),
@@ -434,7 +454,7 @@
             pltpu.VMEM(wide, F32),
             pltpu.VMEM(wide, F32),
             pltpu.VMEM(wide, F32),
-            pltpu.SemaphoreType.DMA((6,)),
+            pltpu.SemaphoreType.DMA((10,)),
             pltpu.SemaphoreType.DMA((3,)),
             pltpu.SemaphoreType.DMA((3,)),
             pltpu.SemaphoreType.DMA((3,)),
@@ -442,10 +462,12 @@
             pltpu.SemaphoreType.DMA((9,)),
             pltpu.SemaphoreType.DMA((9,)),
         ],
-        compiler_params=pltpu.CompilerParams(collective_id=0, has_side_effects=True),
+        compiler_params=pltpu.CompilerParams(
+            collective_id=0, has_side_effects=True, vmem_limit_bytes=16 << 20
+        ),
         name="cycle",
     )
-    return call(
+    arrays = (
         off_cols,
         member_send.reshape(members),
         group_send.reshape(GG),
@@ -457,6 +479,18 @@
         coarse_inv,
         krylov_basis,
     )
+    results = call(*(pltpu.with_memory_space_constraint(v, pltpu.HBM) for v in arrays))
+    hand_out = pl.pallas_call(
+        finish,
+        out_shape=tuple(jax.ShapeDtypeStruct(r.shape, r.dtype) for r in results),
+        in_specs=[vmem] * 4,
+        out_specs=(hbm,) * 4,
+        scratch_shapes=[pltpu.SemaphoreType.DMA((4,))],
+        compiler_params=pltpu.CompilerParams(vmem_limit_bytes=1 << 20),
+        name="finish",
+    )
+    precond, coef, gram, new_block = hand_out(*results)
+    return precond, coef.T, gram, new_block
 
 
 def solution(mesh):

time: 101 us -> 93.6 us (0.927)
  local copies, waits for them, and re-layouts: 5.21 us -> 0 us
  Pallas kernels: 94.4 us -> 92.8 us
    unnamed x3 -> x0, local copies, waits for them, and re-layouts: 3.83 us -> none
    pallas_call x1 -> x2, Pallas kernels: 94.4 us -> 92.8 us  [the longest x1 92.2 us: local(): call(*(pltpu.with_memory_space_constraint(v, pltpu.HBM) for v in arrays))]
    pallas_call x1 -> x0, local copies, waits for them, and re-layouts: 1.38 us -> none  [local(): call(off_cols, member_send.reshape(members), group_send.reshape(GG), agg_...]
where the time goes in v2:
time: 93.6 us; the launch traced here: 93.4 us
  Pallas kernels  92.8 us (99%)
    pallas_call x1, Pallas kernels, local(): call(*(pltpu.with_memory_space_constraint(v, pltpu.HBM) for v in arrays))  92.2 us

profile of v2, /device:TPU:8, one launch (start us, length us, event | category | flops | bytes accessed | tf_op | source)
XLA Modules:
  0.0 93.4 jit_solution(13589234407624945710)
XLA Ops:
  0.6 92.2 %cycle.1 = (bf16[2,8,128]{2,1,0:T(8,128)(2,1)S(1)}, f32[8,32]{1,0:T(8,128)S(1)}, f32[8,8]{1,0:T(8,128)S(1)}, f32[2,8,128]{2,1,0:T(8,128)S(1)}) custom-call(s32[2,8]{1,0:T(2,128)} %cols_hbm.1, s32[64]{0:T(128)} %bitcast.5, s32[4]{0:T(128)} %bitcast.6, s32[2]{0:T(128)} %agg_hbm.1, bf16[2,1024,128]{2,1,0:T(8,128)(2,1)} %bitcast.4, ...), custom_call_target="tpu_custom_call" | custom-call | tf_op jit(solution)/shard_map/cycle/pallas_call | solution.py:482
  92.8 0.6 finish.1

commit v3 on v2

--- a/solution.py
+++ b/solution.py
@@ -15,6 +15,7 @@
 K = 8
 GG = 4
 NX = 4
+NF = 5
 F32 = jnp.float32
 BF16 = jnp.bfloat16
 HIGHEST = lax.Precision.HIGHEST
@@ -45,7 +46,7 @@
     prec_ref, coef_ref, gram_ref, new_ref,
     off_cols, member_send, group_send, agg_map,
     off, diag, smooth, prolong, inv, basis,
-    vals, out_tiles, out_rim, turn_0, turn_1, turn_2, ext_0, ext_1, ext_2,
+    vals, far_tiles, out_tiles, out_rim, turn_0, turn_1, turn_2, ext_0, ext_1, ext_2,
     cx, cz, cg, corr,
     bz, bx, bg, fg, fx, fz,
     c_own, s_own, g_own, b_own, b2_own, b3_own, f_own, f2_own, f3_own,
@@ -60,6 +61,11 @@
     x = lax.rem(m, NX)
     scale_rows = 1.0 / rows_all
 
+    def away(k):
+        return nz // 2 + (k + 1) // 2 * (1 - 2 * (k % 2))
+
+    near = [*(away(k) for k in range(NF, nz - 1)), 0]
+
     def at_member(pz, px):
         return {"group": g, "member": pz * NX + px}
 
@@ -68,6 +74,15 @@
 
     def z_of(k):
         return lax.rem(z + nz // 2 + lax.div(k + 1, 2) * (1 - 2 * lax.rem(k, 2)), nz)
+
+    def each_far(act):
+        def step(k, carry):
+            pz = z_of(k)
+            for px in range(NX):
+                act(k, pz, px)
+            return carry
+
+        lax.fori_loop(0, NF, step, 0)
 
     def each_z(act):
         def step(k, carry):
@@ -85,11 +100,15 @@
         lax.fori_loop(0, groups - 1, step, 0)
 
     barrier = pltpu.get_barrier_semaphore()
-    each_z(
-        lambda pz: pl.semaphore_signal(
-            barrier, inc=1, device_id=at_member(pz, x), device_id_type=MESH
-        )
-    )
+    each_far(
+        lambda k, pz, px: pl.semaphore_signal(
+            barrier, inc=1, device_id=at_member(pz, px), device_id_type=MESH
+        )
+    )
+    for dz in near[:-1]:
+        pl.semaphore_signal(
+            barrier, inc=1, device_id=at_member(lax.rem(z + dz, nz), x), device_id_type=MESH
+        )
     for d in range(1, NX):
         pl.semaphore_signal(barrier, inc=1, device_id=at_member(z, xs[d]), device_id_type=MESH)
     each_group(
@@ -128,17 +147,29 @@
             vals[r, t] = tiles[t]
             ext[r][t] = tiles[t]
 
-        def step(pz, carry):
+        for k in range(NF):
+            pz = lax.rem(z + away(k), nz)
             for px in range(NX):
-                out_tiles[r, px, pz] = vals[r, member_send[pz * NX + px]]
-            turn[r][x, pz] = vals[r, member_send[pz * NX + x]]
-            return carry
-
-        lax.fori_loop(0, nz, step, 0, unroll=True)
+                far_tiles[r, k, px] = vals[r, member_send[pz * NX + px]]
+        for j, dz in enumerate(near):
+            pz = lax.rem(z + dz, nz)
+            for px in range(NX):
+                out_tiles[r, px, j] = vals[r, member_send[pz * NX + px]]
+            turn[r][x, j] = vals[r, member_send[pz * NX + x]]
         for s in range(GG):
             out_rim[r, s] = vals[r, group_send[s]]
 
     def send_tiles(r):
+        each_far(
+            lambda k, pz, px: pltpu.make_async_remote_copy(
+                src_ref=far_tiles.at[r, k, px],
+                dst_ref=ext[r].at[TD + m],
+                send_sem=ex_send.at[r],
+                recv_sem=ex_recv.at[r],
+                device_id=at_member(pz, px),
+                device_id_type=MESH,
+            ).start()
+        )
         for d in x_order:
             pltpu.make_async_remote_copy(
                 src_ref=out_tiles.at[r, xs[d]],
@@ -164,19 +195,17 @@
         view = turn[r].at[pl.ds(0, NX - 1)]
         pltpu.make_async_copy(view, view, turn_recv.at[r]).wait()
 
-        def act(pz):
+        for j, dz in enumerate(near[:-1]):
             pltpu.make_async_remote_copy(
-                src_ref=turn[r].at[:, pz],
+                src_ref=turn[r].at[:, j],
                 dst_ref=ext[r].at[pl.ds(TD + z * NX, NX)],
                 send_sem=ex_send.at[r],
                 recv_sem=ex_recv.at[r],
-                device_id=at_member(pz, x),
+                device_id=at_member(lax.rem(z + dz, nz), x),
                 device_id_type=MESH,
             ).start()
-
-        each_z(act)
         for px in range(NX):
-            ext[r][TD + z * NX + px] = turn[r][px, z]
+            ext[r][TD + z * NX + px] = turn[r][px, len(near) - 1]
         view = ext[r].at[pl.ds(0, moved)]
         pltpu.make_async_copy(view, view, ex_recv.at[r]).wait()
 
@@ -248,7 +277,7 @@
     for i in (2, 3, 4, 5, 8, 9):
         loads[i].wait()
 
-    pl.semaphore_wait(barrier, nz + NX + groups - 3)
+    pl.semaphore_wait(barrier, NF * NX + len(near) + NX + groups - 3)
     send_tiles(0)
     take_tiles(0)
 
@@ -427,11 +456,12 @@
             pltpu.VMEM((groups * CTG * TILE, CTG * TILE), BF16),
             pltpu.VMEM((TD, NB, TILE), BF16),
             pltpu.VMEM((3, TD, NVEC, TILE), BF16),
-            pltpu.VMEM((3, NX, nz, NVEC, TILE), BF16),
+            pltpu.VMEM((3, NF, NX, NVEC, TILE), BF16),
+            pltpu.VMEM((3, NX, nz - NF, NVEC, TILE), BF16),
             pltpu.VMEM((3, GG, NVEC, TILE), BF16),
-            pltpu.VMEM((NX, nz, NVEC, TILE), BF16),
-            pltpu.VMEM((NX, nz, NVEC, TILE), BF16),
-            pltpu.VMEM((NX, nz, NVEC, TILE), BF16),
+            pltpu.VMEM((NX, nz - NF, NVEC, TILE), BF16),
+            pltpu.VMEM((NX, nz - NF, NVEC, TILE), BF16),
+            pltpu.VMEM((NX, nz - NF, NVEC, TILE), BF16),
             pltpu.VMEM((slots, NVEC, TILE), BF16),
             pltpu.VMEM((slots, NVEC, TILE), BF16),
             pltpu.VMEM((slots, NVEC, TILE), BF16),

time: 93.6 us -> 88.1 us (0.941)
  Pallas kernels: 92.8 us -> 87 us
    pallas_call x1, Pallas kernels: 92.2 us -> 86.4 us  [local(): call(*(pltpu.with_memory_space_constraint(v, pltpu.HBM) for v in arrays))]
where the time goes in v3:
time: 88.1 us; the launch traced here: 87.7 us
  Pallas kernels  87 us (99%)
    pallas_call x1, Pallas kernels, local(): call(*(pltpu.with_memory_space_constraint(v, pltpu.HBM) for v in arrays))  86.4 us

profile of v3, /device:TPU:8, one launch (start us, length us, event | category | flops | bytes accessed | tf_op | source)
XLA Modules:
  0.0 87.7 jit_solution(12096269272666222764)
XLA Ops:
  0.6 86.4 %cycle.1 = (bf16[2,8,128]{2,1,0:T(8,128)(2,1)S(1)}, f32[8,32]{1,0:T(8,128)S(1)}, f32[8,8]{1,0:T(8,128)S(1)}, f32[2,8,128]{2,1,0:T(8,128)S(1)}) custom-call(s32[2,8]{1,0:T(2,128)} %cols_hbm.1, s32[64]{0:T(128)} %bitcast.5, s32[4]{0:T(128)} %bitcast.6, s32[2]{0:T(128)} %agg_hbm.1, bf16[2,1024,128]{2,1,0:T(8,128)(2,1)} %bitcast.4, ...), custom_call_target="tpu_custom_call" | custom-call | tf_op jit(solution)/shard_map/cycle/pallas_call | solution.py:512
  87.0 0.6 finish.1

commit v4 on v3

--- a/solution.py
+++ b/solution.py
@@ -48,7 +48,7 @@
     off, diag, smooth, prolong, inv, basis,
     vals, far_tiles, out_tiles, out_rim, turn_0, turn_1, turn_2, ext_0, ext_1, ext_2,
     cx, cz, cg, corr,
-    bz, bx, bg, fg, fx, fz,
+    bz, bx, bg, fg, fx, ff, fz, fold,
     c_own, s_own, g_own, b_own, b2_own, b3_own, f_own, f2_own, f3_own,
     load_sem, turn_send, turn_recv, ex_send, ex_recv, st_send, st_recv,
 ):
@@ -356,14 +356,11 @@
     send_g(6, f_own, fg)
     take(6, fg, groups - 1)
     part = total(fg, groups)
+    part = part[:3] + pltpu.roll(part[3:6], 40, 1) + pltpu.roll(part[5:], 80, 1)
     f2_own[...] = part
     fx[x] = part
+    each_far(lambda k, pz, px: push(9, f2_own, ff.at[m], at_member(pz, px)))
     send_x(7, f2_own, fx)
-    take(7, fx, NX - 1)
-    part = total(fx, NX)
-    f3_own[...] = part
-    fz[z] = part
-    send_z(8, f3_own, fz)
     take(5, bg, groups - 1)
     packed = total(bg, groups)
     basis_total = jnp.concatenate(
@@ -377,8 +374,27 @@
     wide_rows = lax.broadcasted_iota(jnp.int32, (NB, TILE), 0)
     basis_total = jnp.where(wide_lanes < NB, basis_total, 0.0)
     mirror = jnp.where(wide_rows == wide_lanes, 2.0, 0.0) - basis_total
-    take(8, fz, nz - 1)
-    part = total(fz, nz)
+    take(7, fx, NX - 1)
+    part = total(fx, NX)
+    f3_own[...] = part
+    for dz in near[:-1]:
+        push(8, f3_own, fz.at[z], at_member(lax.rem(z + dz, nz), x))
+    fz[z] = part
+    take(9, ff, NF * NX)
+    for k in range(NF):
+        pz = lax.rem(z + away(k), nz)
+        fz_sum = ff[pz * NX]
+        for px in range(1, NX):
+            fz_sum = fz_sum + ff[pz * NX + px]
+        fold[pz] = fz_sum
+    take(8, fz, len(near) - 1)
+    fold[z] = part
+    for dz in near[:-1]:
+        pz = lax.rem(z + dz, nz)
+        fold[pz] = fz[pz]
+    part = total(fold, nz)
+    whole = jnp.concatenate([part, pltpu.roll(part, 88, 1), pltpu.roll(part, 48, 1)[1:]], axis=0)
+    part = whole
 
     coef = jnp.where(lanes < NB, part, 0.0)
     square = pltpu.roll(part, TILE - NB, 1)
@@ -410,7 +426,7 @@
     for i, (buf, count) in enumerate(
         (
             (cx, NX), (cz, nz), (cg, groups), (bz, nz), (bx, NX), (bg, groups),
-            (fg, groups), (fx, NX), (fz, nz),
+            (fg, groups), (fx, NX), (fz, len(near)), (ff, NF * NX + 1),
         )
     ):
         view = buf.at[pl.ds(0, count - 1)]
@@ -473,8 +489,10 @@
             pltpu.VMEM((NX, *wide), F32),
             pltpu.VMEM((groups, *wide), F32),
             pltpu.VMEM((groups, *wide), F32),
-            pltpu.VMEM((NX, *wide), F32),
-            pltpu.VMEM((nz, *wide), F32),
+            pltpu.VMEM((NX, 3, TILE), F32),
+            pltpu.VMEM((members, 3, TILE), F32),
+            pltpu.VMEM((nz, 3, TILE), F32),
+            pltpu.VMEM((nz, 3, TILE), F32),
             pltpu.VMEM((CTG * NVEC, TILE), F32),
             pltpu.VMEM((CTG * NVEC, TILE), F32),
             pltpu.VMEM((CTG, NVEC, TILE), BF16),
@@ -482,15 +500,15 @@
             pltpu.VMEM(wide, F32),
             pltpu.VMEM(wide, F32),
             pltpu.VMEM(wide, F32),
-            pltpu.VMEM(wide, F32),
-            pltpu.VMEM(wide, F32),
+            pltpu.VMEM((3, TILE), F32),
+            pltpu.VMEM((3, TILE), F32),
             pltpu.SemaphoreType.DMA((10,)),
             pltpu.SemaphoreType.DMA((3,)),
             pltpu.SemaphoreType.DMA((3,)),
             pltpu.SemaphoreType.DMA((3,)),
             pltpu.SemaphoreType.DMA((3,)),
-            pltpu.SemaphoreType.DMA((9,)),
-            pltpu.SemaphoreType.DMA((9,)),
+            pltpu.SemaphoreType.DMA((10,)),
+            pltpu.SemaphoreType.DMA((10,)),
         ],
         compiler_params=pltpu.CompilerParams(
             collective_id=0, has_side_effects=True, vmem_limit_bytes=16 << 20

time: 88.1 us -> 87.1 us (0.989)
  no operation moved by 1% of the time
where the time goes in v4:
time: 87.1 us; the launch traced here: 86.9 us
  Pallas kernels  86.2 us (99%)
    pallas_call x1, Pallas kernels, local(): call(*(pltpu.with_memory_space_constraint(v, pltpu.HBM) for v in arrays))  85.6 us

profile of v4, /device:TPU:8, one launch (start us, length us, event | category | flops | bytes accessed | tf_op | source)
XLA Modules:
  0.0 86.9 jit_solution(16944065492760518103)
XLA Ops:
  0.6 85.6 %cycle.1 = (bf16[2,8,128]{2,1,0:T(8,128)(2,1)S(1)}, f32[8,32]{1,0:T(8,128)S(1)}, f32[8,8]{1,0:T(8,128)S(1)}, f32[2,8,128]{2,1,0:T(8,128)S(1)}) custom-call(s32[2,8]{1,0:T(2,128)} %cols_hbm.1, s32[64]{0:T(128)} %bitcast.5, s32[4]{0:T(128)} %bitcast.6, s32[2]{0:T(128)} %agg_hbm.1, bf16[2,1024,128]{2,1,0:T(8,128)(2,1)} %bitcast.4, ...), custom_call_target="tpu_custom_call" | custom-call | tf_op jit(solution)/shard_map/cycle/pallas_call | solution.py:530
  86.2 0.6 finish.1
